TPU v7x, 8 devices: a whole 2x2x1 slice. The times are simulated.
8 devices in a mesh: dp: 1 (over z), ep: 8 (over y, x, core).
Axes of the slice: x: 2, y: 2, z: 1, core: 2. Of those that a mesh axis runs over, the one named last changes fastest.
Arguments:
- resid_in: bfloat16 [2, 32, 384, 2048], P(None, ('dp', 'ep'))
- expert_idx: int32 [2, 32, 384, 6], P(None, ('dp', 'ep'))
- expert_slot: int32 [2, 32, 384, 6], P(None, ('dp', 'ep'))
- w_query: bfloat16 [2048, 16, 128], replicated
- w_key: bfloat16 [2048, 16, 128], replicated
- w_value: bfloat16 [2048, 16, 128], replicated
- w_out: bfloat16 [16, 128, 2048], replicated
- w_gate: bfloat16 [2048, 10944], replicated
- w_up: bfloat16 [2048, 10944], replicated
- w_down: bfloat16 [10944, 2048], replicated
- w_router: bfloat16 [2048, 64], replicated
- norm_attn: bfloat16 [2048], replicated
- norm_ffn: bfloat16 [2048], replicated
- norm_moe: bfloat16 [2048], replicated
- expert_gate: bfloat16 [64, 2048, 1408], P('ep')
- expert_up: bfloat16 [64, 2048, 1408], P('ep')
- expert_down: bfloat16 [64, 1408, 2048], P('ep')
Outputs:
- output: bfloat16 [2, 32, 384, 2048], P(None, ('dp', 'ep'))
All inputs are finite; a program needn't handle non-finite values.
Results may differ from a plain program's by a relative error of at most 0.00994233.
Values are sent between devices in bfloat16 or wider.
A program may use at most 1.25 GiB of HBM per device.

v0:
```python
import jax
import jax.numpy as jnp
from jax import lax
from jax.sharding import PartitionSpec as P, NamedSharding

EPS = 1e-6
ROPE_BASE = 10000.0
CAP_FACTOR = 2


def rms_norm(values, scale):
    widened = values.astype(jnp.float32)
    mean_sq = jnp.mean(widened * widened, axis=-1, keepdims=True)
    return (widened * lax.rsqrt(mean_sq + EPS) * scale.astype(jnp.float32)).astype(jnp.bfloat16)


def rotary(values):
    seq_len = values.shape[-3]
    head_dim = values.shape[-1]
    half_dim = head_dim // 2
    freqs = ROPE_BASE ** (-jnp.arange(half_dim, dtype=jnp.float32) * 2.0 / head_dim)
    angles = jnp.arange(seq_len, dtype=jnp.float32)[:, None] * freqs[None, :]
    cosine = jnp.cos(angles)[:, None, :]
    sine = jnp.sin(angles)[:, None, :]
    first = values[..., :half_dim]
    second = values[..., half_dim:]
    return jnp.concatenate([first * cosine - second * sine, second * cosine + first * sine], axis=-1)


def dense_branch(resid, norm_attn, w_query, w_key, w_value, w_out, norm_ffn, w_gate, w_up, w_down):
    batch, seq_len = resid.shape[0], resid.shape[1]
    heads, head_dim = w_query.shape[1], w_query.shape[2]
    kv_heads = w_key.shape[1]
    normed = rms_norm(resid, norm_attn)
    queries = rotary(jnp.einsum('bsd,dhe->bshe', normed, w_query, preferred_element_type=jnp.float32)).astype(jnp.bfloat16)
    keys_rot = rotary(jnp.einsum('bsd,dhe->bshe', normed, w_key, preferred_element_type=jnp.float32)).astype(jnp.bfloat16)
    values_in = jnp.einsum('bsd,dhe->bshe', normed, w_value, preferred_element_type=jnp.float32).astype(jnp.bfloat16)
    grouped = queries.reshape(batch, seq_len, kv_heads, heads // kv_heads, head_dim)
    scores = jnp.einsum('bqgre,bkge->bgrqk', grouped, keys_rot, preferred_element_type=jnp.float32) * (head_dim ** -0.5)
    causal = jnp.arange(seq_len)[:, None] >= jnp.arange(seq_len)[None, :]
    probs = jax.nn.softmax(jnp.where(causal, scores, -1e30), axis=-1).astype(jnp.bfloat16)
    attended = jnp.einsum('bgrqk,bkge->bqgre', probs, values_in, preferred_element_type=jnp.float32).astype(jnp.bfloat16)
    attn_out = jnp.einsum('bshe,hed->bsd', attended.reshape(batch, seq_len, heads, head_dim), w_out, preferred_element_type=jnp.float32)
    after_attn = (resid.astype(jnp.float32) + attn_out).astype(jnp.bfloat16)
    normed_ffn = rms_norm(after_attn, norm_ffn)
    gate_act = jnp.einsum('bsd,df->bsf', normed_ffn, w_gate, preferred_element_type=jnp.float32)
    up_act = jnp.einsum('bsd,df->bsf', normed_ffn, w_up, preferred_element_type=jnp.float32)
    hidden = (jax.nn.silu(gate_act) * up_act).astype(jnp.bfloat16)
    down_act = jnp.einsum('bsf,fd->bsd', hidden, w_down, preferred_element_type=jnp.float32)
    return after_attn.astype(jnp.float32) + down_act


def route(tokens_in, norm_moe, w_router, route_ids):
    normed = rms_norm(tokens_in, norm_moe)
    logits = jnp.dot(normed, w_router, preferred_element_type=jnp.float32)
    picked = jnp.take_along_axis(logits, route_ids, axis=1)
    return normed, jax.nn.softmax(picked, axis=-1)


def expert_ffn(rows_in, expert_gate, expert_up, expert_down):
    gate_act = jnp.einsum('lrd,ldf->lrf', rows_in, expert_gate, preferred_element_type=jnp.float32)
    up_act = jnp.einsum('lrd,ldf->lrf', rows_in, expert_up, preferred_element_type=jnp.float32)
    hidden = (jax.nn.silu(gate_act) * up_act).astype(jnp.bfloat16)
    return jnp.einsum('lrf,lfd->lrd', hidden, expert_down, preferred_element_type=jnp.float32).astype(jnp.bfloat16)


def solution(mesh):
    group_size = mesh.shape['ep']
    tok_spec = P(None, ('dp', 'ep'), None, None)
    rep_one = P(None)
    rep_two = P(None, None)
    rep_three = P(None, None, None)
    expert_spec = P('ep', None, None)

    def local_program(resid_in, expert_idx, expert_slot, w_query, w_key, w_value, w_out, w_gate, w_up, w_down, w_router, norm_attn, norm_ffn, norm_moe, expert_gate, expert_up, expert_down):
        micro_count, seqs, seq_len, width = resid_in.shape
        tokens = seqs * seq_len
        choices = expert_idx.shape[-1]
        local_experts = expert_gate.shape[0]
        capacity = CAP_FACTOR * tokens * choices // (local_experts * group_size)
        buf_rows = local_experts * group_size * capacity
        token_of_copy = jnp.broadcast_to(jnp.arange(tokens, dtype=jnp.int32)[:, None], (tokens, choices)).reshape(-1)
        outputs = []
        for micro in range(micro_count):
            resid = resid_in[micro]
            route_ids = expert_idx[micro].reshape(tokens, choices)
            route_slots = expert_slot[micro].reshape(tokens, choices)
            normed, gates = route(resid.reshape(tokens, width), norm_moe, w_router, route_ids)
            buf_pos = ((route_ids % local_experts) * group_size + route_ids // local_experts) * capacity + route_slots
            source_row = jnp.full((buf_rows,), tokens, jnp.int32).at[buf_pos.reshape(-1)].set(token_of_copy)
            send_buf = jnp.take(normed, source_row, axis=0, mode='fill', fill_value=0).reshape(local_experts, group_size, capacity, width)
            received = lax.all_to_all(send_buf, 'ep', 1, 1, tiled=True)
            expert_out = expert_ffn(received.reshape(local_experts, group_size * capacity, width), expert_gate, expert_up, expert_down)
            returned = lax.all_to_all(expert_out.reshape(local_experts, group_size, capacity, width), 'ep', 1, 1, tiled=True)
            per_copy = jnp.take(returned.reshape(buf_rows, width), buf_pos, axis=0)
            moe_out = jnp.sum(gates[:, :, None] * per_copy.astype(jnp.float32), axis=1)
            dense_out = dense_branch(resid, norm_attn, w_query, w_key, w_value, w_out, norm_ffn, w_gate, w_up, w_down)
            outputs.append((dense_out + moe_out.reshape(seqs, seq_len, width)).astype(jnp.bfloat16))
        return jnp.stack(outputs)

    return jax.shard_map(local_program, mesh=mesh, in_specs=(tok_spec, tok_spec, tok_spec, rep_three, rep_three, rep_three, rep_three, rep_two, rep_two, rep_two, rep_two, rep_one, rep_one, rep_one, expert_spec, expert_spec, expert_spec), out_specs=tok_spec, check_vma=False)
```

profile of v0, /device:TPU:0, one launch (start us, length us, event | category | flops | bytes accessed | tf_op | source)
XLA Modules:
  0.0 4213.4 jit_solution(5071412714386033229)
XLA Ops:
  0.0 1.5 slice_bitcast_fusion.2
  2.4 1.4 slice_bitcast_fusion.3
  5.6 34.2 scatter_custom_fusion.1
  41.1 6.3 fusion.52
  47.5 10.3 fusion.50
  57.8 140.0 %gather_fusion.4 = bf16[18432,2048]{1,0:T(8,128)(2,1)} fusion(bf16[1536,2048]{1,0:T(8,128)(2,1)} %get-tuple-element.27, s32[18432]{0:T(1024)S(1)} %fusion.139), kind=kCustom, calls=%fused_computation.4.clone | custom fusion | bytes 151068672 | tf_op jit(solution)/shard_map/jit(_take)/gather | solution.py:91
  197.8 49.7 %broadcast_select_fusion = bf16[18432,2048]{1,0:T(8,128)(2,1)} fusion(bf16[18432,2048]{1,0:T(8,128)(2,1)} %gather_fusion.4, pred[18432]{0:T(1024)(128)(4,1)S(1)} %copy-done.34), kind=kLoop, calls=%fused_computation.12 | loop fusion | flops 37748736 | bytes 151013376 | tf_op jit(solution)/shard_map/jit(_take)/select_n | solution.py:91
  247.6 49.4 %copy.119 = bf16[8,8,288,2048]{3,2,0,1:T(8,128)(2,1)} copy(bf16[8,8,288,2048]{3,2,1,0:T(8,128)(2,1)} %bitcast.46) | data formatting | bytes 150994944 | tf_op jit(solution)/shard_map/reshape | solution.py:91
  297.1 9.5 all-to-all-start.2
  308.7 34.6 scatter_custom_fusion
  345.2 4.8 fusion.180
  350.8 73.7 %gather_fusion.3 = f32[9216]{0:T(1024)S(1)} fusion(f32[1536,64]{0,1:T(8,128)S(1)} %fusion.180, s32[9216]{0:T(1024)S(1)} %reshape.600), kind=kCustom, calls=%fused_computation.3.clone | custom fusion | bytes 147456 | tf_op jit(solution)/shard_map/jit(take_along_axis)/gather | solution.py:56
  426.2 12.4 copy.88
  439.2 12.3 copy.87
  451.5 140.0 %gather_fusion.1 = bf16[18432,2048]{1,0:T(8,128)(2,1)} fusion(bf16[1536,2048]{1,0:T(8,128)(2,1)} %get-tuple-element.26, s32[18432]{0:T(1024)S(1)} %copy-done.19), kind=kCustom, calls=%fused_computation.1.clone | custom fusion | bytes 151068672 | tf_op jit(solution)/shard_map/jit(_take)/gather | solution.py:91
  591.5 49.5 %broadcast_select_fusion.1 = bf16[18432,2048]{1,0:T(8,128)(2,1)} fusion(bf16[18432,2048]{1,0:T(8,128)(2,1)} %gather_fusion.1, pred[18432]{0:T(1024)(128)(4,1)S(1)} %copy-done.33), kind=kLoop, calls=%fused_computation.13 | loop fusion | flops 37748736 | bytes 151013376 | tf_op jit(solution)/shard_map/jit(_take)/select_n | solution.py:91
  641.0 49.5 %copy.100 = bf16[8,8,288,2048]{3,2,0,1:T(8,128)(2,1)} copy(bf16[8,8,288,2048]{3,2,1,0:T(8,128)(2,1)} %bitcast.22) | data formatting | bytes 150994944 | tf_op jit(solution)/shard_map/reshape | solution.py:91
  692.6 4.8 fusion.178
  697.5 73.7 %gather_fusion = f32[9216]{0:T(1024)S(1)} fusion(f32[1536,64]{0,1:T(8,128)S(1)} %fusion.178, s32[9216]{0:T(1024)S(1)} %reshape.589), kind=kCustom, calls=%fused_computation.clone | custom fusion | bytes 147456 | tf_op jit(solution)/shard_map/jit(take_along_axis)/gather | solution.py:56
  773.1 7.5 fusion.53
  783.8 18.1 fusion.62
  801.9 16.7 fusion.60
  818.6 17.1 fusion.64
  835.8 16.7 fusion.66
  852.5 27.4 subtract_convert_fusion.2
  879.9 18.4 fusion.24
  898.3 31.6 fusion.22
  929.9 16.8 fusion.23
  946.8 31.8 fusion.26
  978.6 22.0 fusion.37
  1000.6 32.1 fusion.28
  1032.7 88.6 %all-to-all-done.2 = bf16[8,8,288,2048]{3,2,0,1:T(8,128)(2,1)} async-done(((bf16[8,8,288,2048]{3,2,0,1:T(8,128)(2,1)}), bf16[8,8,288,2048]{3,2,0,1:T(8,128)(2,1)}, u32[]{:S(2)}, u32[]{:S(2)}) %all-to-all-start.2) | async-done | bytes 75497504 | tf_op jit(solution)/shard_map/all_to_all | solution.py:92
  1121.3 9.6 all-to-all-start
  1130.9 49.6 %copy.120 = bf16[8,8,288,2048]{3,2,1,0:T(8,128)(2,1)} copy(bf16[8,8,288,2048]{3,2,0,1:T(8,128)(2,1)} %all-to-all-done.2) | data formatting | bytes 150994944 | tf_op jit(solution)/shard_map/all_to_all | solution.py:92
  1180.5 127.2 %fusion.181 = f32[8,2304,1408]{2,1,0:T(8,128)} fusion(bf16[8,2304,2048]{2,1,0:T(8,128)(2,1)} %bitcast.47, bf16[8,2048,1408]{2,1,0:T(8,128)(2,1)} %param.37), kind=kOutput, calls=%fused_computation.240 | convolution fusion | flops 106300440576 | bytes 225443840 | tf_op jit(solution)/shard_map/lrd,ldf->lrf/dot_general | solution.py:61
  1307.7 135.3 %fusion.1 = bf16[8,2304,1408]{2,1,0:T(8,128)(2,1)} fusion(bf16[8,2304,2048]{2,1,0:T(8,128)(2,1)} %bitcast.47, bf16[8,2048,1408]{2,1,0:T(8,128)(2,1)} %param.38, f32[8,2304,1408]{2,1,0:T(8,128)} %fusion.181), kind=kOutput, calls=%fused_computation.17 | convolution fusion | flops 106456154112 | bytes 277348352 | tf_op jit(solution)/shard_map/lrd,ldf->lrf/dot_general | solution.py:62
  1443.0 127.5 %convolution_convert_fusion = bf16[8,2304,2048]{2,1,0:T(8,128)(2,1)} fusion(bf16[8,2304,1408]{2,1,0:T(8,128)(2,1)} %fusion.1, bf16[8,1408,2048]{2,1,0:T(8,128)(2,1)} %param.39), kind=kOutput, calls=%fused_computation.18 | convolution fusion | flops 106338189312 | bytes 173539328 | tf_op jit(solution)/shard_map/lrf,lfd->lrd/dot_general | solution.py:64
  1570.5 49.6 %copy.121 = bf16[8,8,288,2048]{3,2,0,1:T(8,128)(2,1)} copy(bf16[8,8,288,2048]{3,2,1,0:T(8,128)(2,1)} %bitcast.48) | data formatting | bytes 150994944 | tf_op jit(solution)/shard_map/reshape | solution.py:94
  1620.1 324.5 %all-to-all-done = bf16[8,8,288,2048]{3,2,0,1:T(8,128)(2,1)} async-done(((bf16[8,8,288,2048]{3,2,0,1:T(8,128)(2,1)}), bf16[8,8,288,2048]{3,2,0,1:T(8,128)(2,1)}, u32[]{:S(2)}, u32[]{:S(2)}) %all-to-all-start) | async-done | bytes 75497504 | tf_op jit(solution)/shard_map/all_to_all | solution.py:92
  1944.6 9.5 all-to-all-start.3
  1954.1 49.4 %copy.101 = bf16[8,8,288,2048]{3,2,1,0:T(8,128)(2,1)} copy(bf16[8,8,288,2048]{3,2,0,1:T(8,128)(2,1)} %all-to-all-done) | data formatting | bytes 150994944 | tf_op jit(solution)/shard_map/all_to_all | solution.py:92
  2003.6 127.2 %fusion.179 = f32[8,2304,1408]{2,1,0:T(8,128)} fusion(bf16[8,2304,2048]{2,1,0:T(8,128)(2,1)} %bitcast.23, bf16[8,2048,1408]{2,1,0:T(8,128)(2,1)} %param.37), kind=kOutput, calls=%fused_computation.238 | convolution fusion | flops 106300440576 | bytes 225443840 | tf_op jit(solution)/shard_map/lrd,ldf->lrf/dot_general | solution.py:61
  2130.8 135.4 %fusion = bf16[8,2304,1408]{2,1,0:T(8,128)(2,1)} fusion(bf16[8,2304,2048]{2,1,0:T(8,128)(2,1)} %bitcast.23, bf16[8,2048,1408]{2,1,0:T(8,128)(2,1)} %param.38, f32[8,2304,1408]{2,1,0:T(8,128)} %fusion.179), kind=kOutput, calls=%fused_computation.16 | convolution fusion | flops 106456154112 | bytes 277348352 | tf_op jit(solution)/shard_map/lrd,ldf->lrf/dot_general | solution.py:62
  2266.2 127.8 %convolution_convert_fusion.1 = bf16[8,2304,2048]{2,1,0:T(8,128)(2,1)} fusion(bf16[8,2304,1408]{2,1,0:T(8,128)(2,1)} %fusion, bf16[8,1408,2048]{2,1,0:T(8,128)(2,1)} %param.39), kind=kOutput, calls=%fused_computation.19 | convolution fusion | flops 106338189312 | bytes 173539328 | tf_op jit(solution)/shard_map/lrf,lfd->lrd/dot_general | solution.py:64
  2393.9 49.4 %copy.102 = bf16[8,8,288,2048]{3,2,0,1:T(8,128)(2,1)} copy(bf16[8,8,288,2048]{3,2,1,0:T(8,128)(2,1)} %bitcast.24) | data formatting | bytes 150994944 | tf_op jit(solution)/shard_map/reshape | solution.py:94
  2443.5 324.4 %all-to-all-done.3 = bf16[8,8,288,2048]{3,2,0,1:T(8,128)(2,1)} async-done(((bf16[8,8,288,2048]{3,2,0,1:T(8,128)(2,1)}), bf16[8,8,288,2048]{3,2,0,1:T(8,128)(2,1)}, u32[]{:S(2)}, u32[]{:S(2)}) %all-to-all-start.3) | async-done | bytes 75497504 | tf_op jit(solution)/shard_map/all_to_all | solution.py:94
  2767.9 9.5 all-to-all-start.1
  2783.5 21.3 fusion.32
  2806.1 79.6 %fusion.6 = f32[4,384,10944]{1,2,0:T(8,128)} fusion(bf16[2048,10944]{0,1:T(8,128)(2,1)} %param.31, bf16[4,384,2048]{2,1,0:T(8,128)(2,1)S(1)} %bitcast.301, f32[4,384]{1,0:T(4,128)S(1)} %add_rsqrt_fusion.1, f32[2048]{0:T(1024)S(1)} %convert_element_type.155), kind=kOutput, calls=%fused_computation.24 | convolution fusion | flops 68866277376 | bytes 118372352 | tf_op jit(solution)/shard_map/bsd,df->bsf/dot_general | solution.py:47
  2885.7 80.5 %fusion.8 = f32[4,384,10944]{1,2,0:T(8,128)} fusion(bf16[2048,10944]{0,1:T(8,128)(2,1)} %param.31, bf16[4,384,2048]{2,1,0:T(8,128)(2,1)} %get-tuple-element.50, f32[2048]{0:T(1024)S(1)} %convert_element_type.155, f32[4,384]{1,0:T(4,128)S(1)} %add_rsqrt_fusion.4), kind=kOutput, calls=%fused_computation.26 | convolution fusion | flops 68866277376 | bytes 118372352 | tf_op jit(solution)/shard_map/bsd,df->bsf/dot_general | solution.py:47
  2966.2 89.5 %multiply_convert_fusion.12 = bf16[4,384,10944]{1,2,0:T(8,128)(2,1)} fusion(f32[4,384,10944]{1,2,0:T(8,128)} %fusion.6, bf16[2048,10944]{0,1:T(8,128)(2,1)} %param.30, bf16[4,384,2048]{2,1,0:T(8,128)(2,1)} %get-tuple-element.48, f32[4,384]{1,0:T(4,128)S(1)} %add_rsqrt_fusion.1, f32[2048]{0:T(1024)S(1)} %convert_element_type.155), kind=kOutput, calls=%fused_computation.14.clone.clone.clone.clone.1 | convolution fusion | flops 68967137280 | bytes 151992320 | tf_op jit(solution)/shard_map/bsd,df->bsf/dot_general | solution.py:46
  3055.7 89.2 %multiply_convert_fusion.13 = bf16[4,384,10944]{1,2,0:T(8,128)(2,1)} fusion(f32[4,384,10944]{1,2,0:T(8,128)} %fusion.8, bf16[2048,10944]{0,1:T(8,128)(2,1)} %param.30, bf16[4,384,2048]{2,1,0:T(8,128)(2,1)} %get-tuple-element.50, f32[2048]{0:T(1024)S(1)} %convert_element_type.155, f32[4,384]{1,0:T(4,128)S(1)} %copy-done.43), kind=kOutput, calls=%fused_computation.15.clone.clone.clone.clone.1 | convolution fusion | flops 68967137280 | bytes 151992320 | tf_op jit(solution)/shard_map/bsd,df->bsf/dot_general | solution.py:46
  3144.9 49.6 %copy.122 = bf16[8,8,288,2048]{3,2,1,0:T(8,128)(2,1)} copy(bf16[8,8,288,2048]{3,2,0,1:T(8,128)(2,1)} %all-to-all-done.3) | data formatting | bytes 150994944 | tf_op jit(solution)/shard_map/all_to_all | solution.py:94
  3194.5 214.7 %gather_fusion.5 = bf16[9216,2048]{1,0:T(8,128)(2,1)} fusion(bf16[18432,2048]{1,0:T(8,128)(2,1)} %bitcast.49, s32[9216]{0:T(1024)S(1)} %copy-done.4), kind=kCustom, calls=%fused_computation.5.clone | custom fusion | bytes 75534336 | tf_op jit(solution)/shard_map/jit(_take)/gather | solution.py:95
  3409.3 58.5 %reshape.609 = bf16[1536,6,2048]{2,1,0:T(8,128)(2,1)} reshape(bf16[9216,2048]{1,0:T(8,128)(2,1)} %gather_fusion.5) | data formatting | bytes 75497472 | tf_op jit(solution)/shard_map/jit(_take)/gather | solution.py:95
  3467.8 123.3 %all-to-all-done.1 = bf16[8,8,288,2048]{3,2,0,1:T(8,128)(2,1)} async-done(((bf16[8,8,288,2048]{3,2,0,1:T(8,128)(2,1)}), bf16[8,8,288,2048]{3,2,0,1:T(8,128)(2,1)}, u32[]{:S(2)}, u32[]{:S(2)}) %all-to-all-start.1) | async-done | bytes 75497504 | tf_op jit(solution)/shard_map/all_to_all | solution.py:94
  3591.1 49.4 %copy.103 = bf16[8,8,288,2048]{3,2,1,0:T(8,128)(2,1)} copy(bf16[8,8,288,2048]{3,2,0,1:T(8,128)(2,1)} %all-to-all-done.1) | data formatting | bytes 150994944 | tf_op jit(solution)/shard_map/all_to_all | solution.py:94
  3640.6 215.0 %gather_fusion.2 = bf16[9216,2048]{1,0:T(8,128)(2,1)} fusion(bf16[18432,2048]{1,0:T(8,128)(2,1)} %bitcast.25, s32[9216]{0:T(1024)S(1)} %copy-done.3), kind=kCustom, calls=%fused_computation.2.clone | custom fusion | bytes 75534336 | tf_op jit(solution)/shard_map/jit(_take)/gather | solution.py:95
  3855.5 58.8 %reshape.598 = bf16[1536,6,2048]{2,1,0:T(8,128)(2,1)} reshape(bf16[9216,2048]{1,0:T(8,128)(2,1)} %gather_fusion.2) | data formatting | bytes 75497472 | tf_op jit(solution)/shard_map/jit(_take)/gather | solution.py:95
  3914.3 58.9 %multiply_reduce_fusion = f32[1536,2048]{1,0:T(8,128)} fusion(bf16[1536,6,2048]{2,1,0:T(8,128)(2,1)} %reshape.609, f32[1536,6]{1,0:T(8,128)S(1)} %copy-done.5, pred[1536,6]{1,0:T(8,128)(4,1)S(1)} %copy-done.12), kind=kLoop, calls=%fused_computation.10 | loop fusion | flops 72351744 | bytes 50377728 | tf_op jit(solution)/shard_map/reduce_sum | solution.py:96
  3973.3 85.2 %fusion.76 = bf16[1,4,384,2048]{3,2,1,0:T(8,128)(2,1)} fusion(f32[4,384,2048]{2,1,0:T(8,128)} %bitcast.280, bf16[4,384,2048]{2,1,0:T(8,128)(2,1)} %get-tuple-element.48, bf16[10944,2048]{1,0:T(8,128)(2,1)} %param.32, bf16[4,384,10944]{1,2,0:T(8,128)(2,1)} %multiply_convert_fusion.12), kind=kOutput, calls=%fused_computation.109 | convolution fusion | flops 68866277376 | bytes 103612416 | tf_op jit(solution)/shard_map/bsf,fd->bsd/dot_general | solution.py:49
  4058.5 58.9 %multiply_reduce_fusion.1 = f32[1536,2048]{1,0:T(8,128)} fusion(bf16[1536,6,2048]{2,1,0:T(8,128)(2,1)} %reshape.598, f32[1536,6]{1,0:T(8,128)S(1)} %copy-done.6, pred[1536,6]{1,0:T(8,128)(4,1)S(1)} %copy-done.13), kind=kLoop, calls=%fused_computation.11 | loop fusion | flops 72351744 | bytes 50377728 | tf_op jit(solution)/shard_map/reduce_sum | solution.py:96
  4117.4 85.0 %fusion.77 = bf16[1,4,384,2048]{3,2,1,0:T(8,128)(2,1)} fusion(f32[4,384,2048]{2,1,0:T(8,128)} %bitcast.281, bf16[4,384,2048]{2,1,0:T(8,128)(2,1)} %get-tuple-element.50, bf16[10944,2048]{1,0:T(8,128)(2,1)} %param.32, bf16[4,384,10944]{1,2,0:T(8,128)(2,1)} %multiply_convert_fusion.13), kind=kOutput, calls=%fused_computation.110 | convolution fusion | flops 68866277376 | bytes 103612416 | tf_op jit(solution)/shard_map/bsf,fd->bsd/dot_general | solution.py:49
  4202.5 10.5 pad_maximum_fusion
  (181 shorter events, 25.5 us)
Async XLA Ops:
  0.0 345.1 %copy-start = (bf16[2048,64]{0,1:T(8,128)(2,1)S(1)}, bf16[2048,64]{0,1:T(8,128)(2,1)}, u32[]{:S(2)}) copy-start(bf16[2048,64]{0,1:T(8,128)(2,1)} %param.33) | copy-start | bytes 786436
  5.3 52.6 %copy-start.37 = (s32[9216]{0:T(1024)}, s32[9216]{0:T(1024)S(1)}, u32[]{:S(2)}) copy-start(s32[9216]{0:T(1024)S(1)} %reshape.568) | copy-start | bytes 110596
  57.8 140.0 %copy-start.34 = (pred[18432]{0:T(1024)(128)(4,1)S(1)}, pred[18432]{0:T(1024)(128)(4,1)}, u32[]{:S(2)}) copy-start(pred[18432]{0:T(1024)(128)(4,1)} %compare_and_fusion) | copy-start | bytes 55300
  297.0 9.5 copy-start.25
  297.0 10.4 copy-start.26
  297.0 47.5 %copy-start.29 = (s32[1,6,4,384]{3,2,1,0:T(4,128)S(1)}, s32[1,6,4,384]{3,2,1,0:T(4,128)}, u32[]{:S(2)}) copy-start(s32[1,6,4,384]{3,2,1,0:T(4,128)} %get-tuple-element.39) | copy-start | bytes 110596
  297.0 48.1 %copy-start.30 = (s32[1,6,4,384]{3,2,1,0:T(4,128)S(1)}, s32[1,6,4,384]{3,2,1,0:T(4,128)}, u32[]{:S(2)}) copy-start(s32[1,6,4,384]{3,2,1,0:T(4,128)} %get-tuple-element.35) | copy-start | bytes 110596
  297.1 824.2 %all-to-all-start.2 = ((bf16[8,8,288,2048]{3,2,0,1:T(8,128)(2,1)}), bf16[8,8,288,2048]{3,2,0,1:T(8,128)(2,1)}, u32[]{:S(2)}, u32[]{:S(2)}) async-start(bf16[8,8,288,2048]{3,2,0,1:T(8,128)(2,1)} %copy.119), calls=%async_computation.2 | async-start | bytes 150994944 | tf_op jit(solution)/shard_map/all_to_all | solution.py:92
  345.1 4.8 copy-start.10
  424.6 14.1 copy-start.48
  438.6 12.9 copy-start.19
  451.5 140.0 %copy-start.33 = (pred[18432]{0:T(1024)(128)(4,1)S(1)}, pred[18432]{0:T(1024)(128)(4,1)}, u32[]{:S(2)}) copy-start(pred[18432]{0:T(1024)(128)(4,1)} %compare_and_fusion.1) | copy-start | bytes 55300
  641.0 49.5 %copy-start.27 = (s32[1,6,4,384]{3,2,1,0:T(4,128)S(1)}, s32[1,6,4,384]{3,2,1,0:T(4,128)}, u32[]{:S(2)}) copy-start(s32[1,6,4,384]{3,2,1,0:T(4,128)} %get-tuple-element.38) | copy-start | bytes 110596
  641.0 50.1 %copy-start.28 = (s32[1,6,4,384]{3,2,1,0:T(4,128)S(1)}, s32[1,6,4,384]{3,2,1,0:T(4,128)}, u32[]{:S(2)}) copy-start(s32[1,6,4,384]{3,2,1,0:T(4,128)} %get-tuple-element.34) | copy-start | bytes 110596
  691.2 0.6 copy-start.7
  697.4 74.9 %copy-start.11 = (s32[1,6,4,384]{3,1,2,0:T(8,128)S(1)}, s32[1,6,4,384]{3,1,2,0:T(8,128)}, u32[]{:S(2)}) copy-start(s32[1,6,4,384]{3,1,2,0:T(8,128)} %copy-done.10) | copy-start | bytes 110596
  697.4 74.9 %copy-start.16 = (f32[1536,6]{0,1:T(8,128)S(1)}, f32[1536,6]{0,1:T(8,128)}, u32[]{:S(2)}) copy-start(f32[1536,6]{0,1:T(8,128)} %copy.114) | copy-start | bytes 110596
  697.4 74.9 %copy-start.8 = (s32[1,6,4,384]{3,1,2,0:T(8,128)S(1)}, s32[1,6,4,384]{3,1,2,0:T(8,128)}, u32[]{:S(2)}) copy-start(s32[1,6,4,384]{3,1,2,0:T(8,128)} %copy-done.7) | copy-start | bytes 110596
  771.2 10.6 copy-start.23
  771.2 11.9 copy-start.24
  771.2 12.6 copy-start.39
  772.2 29.6 copy-start.14
  772.2 11.5 copy-start.2
  772.4 29.4 copy-start.31
  773.1 28.8 slice-start.2
  780.6 38.0 copy-start.46
  780.6 55.2 %copy-start.44 = (f32[4,384]{1,0:T(4,128)}, f32[4,384]{1,0:T(4,128)S(1)}, u32[]{:S(2)}) copy-start(f32[4,384]{1,0:T(4,128)S(1)} %get-tuple-element.54) | copy-start | bytes 18436
  783.7 18.1 slice-start.3
  783.7 34.9 slice-start
  801.9 16.8 slice-start.1
  835.8 16.7 copy-start.17
  835.8 16.7 copy-start.18
  898.3 31.6 copy-start.50
  929.9 16.9 copy-start.40
  929.9 16.9 copy-start.47
  978.6 22.0 copy-start.45
  978.6 22.0 copy-start.51
  978.6 22.0 copy-start.52
  1121.3 823.3 %all-to-all-start = ((bf16[8,8,288,2048]{3,2,0,1:T(8,128)(2,1)}), bf16[8,8,288,2048]{3,2,0,1:T(8,128)(2,1)}, u32[]{:S(2)}, u32[]{:S(2)}) async-start(bf16[8,8,288,2048]{3,2,0,1:T(8,128)(2,1)} %copy.100), calls=%async_computation | async-start | bytes 150994944 | tf_op jit(solution)/shard_map/all_to_all | solution.py:92
  1944.6 823.3 %all-to-all-start.3 = ((bf16[8,8,288,2048]{3,2,0,1:T(8,128)(2,1)}), bf16[8,8,288,2048]{3,2,0,1:T(8,128)(2,1)}, u32[]{:S(2)}, u32[]{:S(2)}) async-start(bf16[8,8,288,2048]{3,2,0,1:T(8,128)(2,1)} %copy.121), calls=%async_computation.3 | async-start | bytes 150994944 | tf_op jit(solution)/shard_map/all_to_all | solution.py:94
  2443.4 334.0 %copy-start.9 = (s32[1,6,4,384]{3,1,2,0:T(8,128)S(1)}, s32[1,6,4,384]{3,1,2,0:T(8,128)}, u32[]{:S(2)}) copy-start(s32[1,6,4,384]{3,1,2,0:T(8,128)} %copy-done.7) | copy-start | bytes 110596
  2443.4 334.0 %copy-start.15 = (f32[1536,6]{0,1:T(8,128)S(1)}, f32[1536,6]{0,1:T(8,128)}, u32[]{:S(2)}) copy-start(f32[1536,6]{0,1:T(8,128)} %copy-done.14) | copy-start | bytes 110596
  2443.4 334.0 %copy-start.32 = (f32[1536]{0:T(1024)S(1)}, f32[1536]{0:T(1024)}, u32[]{:S(2)}) copy-start(f32[1536]{0:T(1024)} %copy-done.31) | copy-start | bytes 18436
  2443.4 334.0 %copy-start.38 = (f32[1536]{0:T(1024)S(1)}, f32[1536]{0:T(1024)}, u32[]{:S(2)}) copy-start(f32[1536]{0:T(1024)} %fusion.157) | copy-start | bytes 18436
  2443.4 334.0 %copy-start.21 = (s32[1536,6]{0,1:T(8,128)S(1)}, s32[1536,6]{0,1:T(8,128)}, u32[]{:S(2)}) copy-start(s32[1536,6]{0,1:T(8,128)} %get-tuple-element.17) | copy-start | bytes 110596
  2443.4 334.9 %copy-start.22 = (f32[1536,6]{0,1:T(8,128)S(1)}, f32[1536,6]{0,1:T(8,128)}, u32[]{:S(2)}) copy-start(f32[1536,6]{0,1:T(8,128)} %fusion.158) | copy-start | bytes 110596
  2443.4 336.1 %copy-start.36 = (pred[1536,6]{0,1:T(8,128)(4,1)S(1)}, pred[1536,6]{0,1:T(8,128)(4,1)}, u32[]{:S(2)}) copy-start(pred[1536,6]{0,1:T(8,128)(4,1)} %get-tuple-element.16) | copy-start | bytes 27652
  2443.4 337.1 %copy-start.49 = (bf16[2048]{0:T(1024)(128)(2,1)S(1)}, bf16[2048]{0:T(1024)(128)(2,1)}, u32[]{:S(2)}) copy-start(bf16[2048]{0:T(1024)(128)(2,1)} %param.35) | copy-start | bytes 12292
  2443.5 337.0 %copy-start.20 = (s32[1536,6]{0,1:T(8,128)S(1)}, s32[1536,6]{0,1:T(8,128)}, u32[]{:S(2)}) copy-start(s32[1536,6]{0,1:T(8,128)} %get-tuple-element.15) | copy-start | bytes 110596
  2443.5 339.1 %copy-start.35 = (pred[1536,6]{0,1:T(8,128)(4,1)S(1)}, pred[1536,6]{0,1:T(8,128)(4,1)}, u32[]{:S(2)}) copy-start(pred[1536,6]{0,1:T(8,128)(4,1)} %get-tuple-element.14) | copy-start | bytes 27652
  2443.5 340.1 %copy-start.41 = (f32[4,384]{1,0:T(4,128)S(1)}, f32[4,384]{1,0:T(4,128)}, u32[]{:S(2)}) copy-start(f32[4,384]{1,0:T(4,128)} %get-tuple-element.47) | copy-start | bytes 18436
  2767.9 823.2 %all-to-all-start.1 = ((bf16[8,8,288,2048]{3,2,0,1:T(8,128)(2,1)}), bf16[8,8,288,2048]{3,2,0,1:T(8,128)(2,1)}, u32[]{:S(2)}, u32[]{:S(2)}) async-start(bf16[8,8,288,2048]{3,2,0,1:T(8,128)(2,1)} %copy.102), calls=%async_computation.1 | async-start | bytes 150994944 | tf_op jit(solution)/shard_map/all_to_all | solution.py:94
  2777.7 28.3 slice-start.4
  2783.5 22.5 slice-start.5
  2804.8 80.9 %copy-start.42 = (f32[4,384]{1,0:T(4,128)}, f32[4,384]{1,0:T(4,128)S(1)}, u32[]{:S(2)}) copy-start(f32[4,384]{1,0:T(4,128)S(1)} %add_rsqrt_fusion.4) | copy-start | bytes 18436
  2966.2 89.5 %copy-start.43 = (f32[4,384]{1,0:T(4,128)S(1)}, f32[4,384]{1,0:T(4,128)}, u32[]{:S(2)}) copy-start(f32[4,384]{1,0:T(4,128)} %copy-done.42) | copy-start | bytes 18436
  3144.9 49.6 %copy-start.4 = (s32[9216]{0:T(1024)S(1)}, s32[9216]{0:T(1024)}, u32[]{:S(2)}) copy-start(s32[9216]{0:T(1024)} %broadcast_clamp_fusion) | copy-start | bytes 110596
  3467.8 172.7 %copy-start.3 = (s32[9216]{0:T(1024)S(1)}, s32[9216]{0:T(1024)}, u32[]{:S(2)}) copy-start(s32[9216]{0:T(1024)} %broadcast_clamp_fusion.1) | copy-start | bytes 110596
  3855.5 58.8 %copy-start.5 = (f32[1536,6]{1,0:T(8,128)S(1)}, f32[1536,6]{1,0:T(8,128)}, u32[]{:S(2)}) copy-start(f32[1536,6]{1,0:T(8,128)} %copy.115) | copy-start | bytes 110596
  3855.5 58.8 %copy-start.12 = (pred[1536,6]{1,0:T(8,128)(4,1)S(1)}, pred[1536,6]{1,0:T(8,128)(4,1)}, u32[]{:S(2)}) copy-start(pred[1536,6]{1,0:T(8,128)(4,1)} %copy.116) | copy-start | bytes 27652
  3973.3 85.2 %copy-start.6 = (f32[1536,6]{1,0:T(8,128)S(1)}, f32[1536,6]{1,0:T(8,128)}, u32[]{:S(2)}) copy-start(f32[1536,6]{1,0:T(8,128)} %copy.96) | copy-start | bytes 110596
  3973.3 85.2 %copy-start.13 = (pred[1536,6]{1,0:T(8,128)(4,1)S(1)}, pred[1536,6]{1,0:T(8,128)(4,1)}, u32[]{:S(2)}) copy-start(pred[1536,6]{1,0:T(8,128)(4,1)} %copy.97) | copy-start | bytes 27652
  4117.4 95.5 %copy-start.1 = (bf16[2048,64]{0,1:T(8,128)(2,1)S(1)}, bf16[2048,64]{0,1:T(8,128)(2,1)}, u32[]{:S(2)}) copy-start(bf16[2048,64]{0,1:T(8,128)(2,1)} %param.33) | copy-start | bytes 786436
where the time goes:
time: 4230 us; the launch traced here: 4210 us
  matrix products  1530 us (36%)
  local copies, waits for them, and re-layouts  1480 us (35%)
  waiting for transfers between devices  861 us (20%)
  other arithmetic  305 us (7%)
    gather x4, local copies, waits for them, and re-layouts, local_program(): per_copy = jnp.take(returned.reshape(buf_rows, width), buf_pos, axis=0)  547 us
    all_to_all x2, waiting for transfers between devices, local_program(): lax.all_to_all(expert_out.reshape(local_experts, group_size, capacity, wi...  448 us
    all_to_all x2, waiting for transfers between devices, local_program(): received = lax.all_to_all(send_buf, 'ep', 1, 1, tiled=True)  413 us
    gather x2, local copies, waits for them, and re-layouts, local_program(): jnp.take(normed, source_row, axis=0, mode='fill', fill_value=0)  280 us
    dot_general x2, matrix products, expert_ffn(): jnp.einsum('lrd,ldf->lrf', rows_in, expert_up, preferred_element_type=jnp...  271 us
    dot_general x2, matrix products, expert_ffn(): jnp.einsum('lrf,lfd->lrd', hidden, expert_down, preferred_element_type=jn...  255 us
    dot_general x2, matrix products, expert_ffn(): jnp.einsum('lrd,ldf->lrf', rows_in, expert_gate, preferred_element_type=j...  254 us
    dot_general x2, matrix products, dense_branch(): jnp.einsum('bsd,df->bsf', normed_ffn, w_gate, preferred_element_type=jnp....  179 us
  transfers between devices with their start and end apart: 4, of which 4 were waited for; matrix products, arithmetic and copies ran while one was open for 57% of the time, Pallas kernels for 0%

commit v1 on v0

--- a/solution.py
+++ b/solution.py
@@ -1,11 +1,12 @@
 import jax
 import jax.numpy as jnp
 from jax import lax
-from jax.sharding import PartitionSpec as P, NamedSharding
+from jax.sharding import PartitionSpec as P
 
 EPS = 1e-6
 ROPE_BASE = 10000.0
 CAP_FACTOR = 2
+NEG = -1e30
 
 
 def rms_norm(values, scale):
@@ -38,7 +39,7 @@
     grouped = queries.reshape(batch, seq_len, kv_heads, heads // kv_heads, head_dim)
     scores = jnp.einsum('bqgre,bkge->bgrqk', grouped, keys_rot, preferred_element_type=jnp.float32) * (head_dim ** -0.5)
     causal = jnp.arange(seq_len)[:, None] >= jnp.arange(seq_len)[None, :]
-    probs = jax.nn.softmax(jnp.where(causal, scores, -1e30), axis=-1).astype(jnp.bfloat16)
+    probs = jax.nn.softmax(jnp.where(causal, scores, NEG), axis=-1).astype(jnp.bfloat16)
     attended = jnp.einsum('bgrqk,bkge->bqgre', probs, values_in, preferred_element_type=jnp.float32).astype(jnp.bfloat16)
     attn_out = jnp.einsum('bshe,hed->bsd', attended.reshape(batch, seq_len, heads, head_dim), w_out, preferred_element_type=jnp.float32)
     after_attn = (resid.astype(jnp.float32) + attn_out).astype(jnp.bfloat16)
@@ -48,13 +49,6 @@
     hidden = (jax.nn.silu(gate_act) * up_act).astype(jnp.bfloat16)
     down_act = jnp.einsum('bsf,fd->bsd', hidden, w_down, preferred_element_type=jnp.float32)
     return after_attn.astype(jnp.float32) + down_act
-
-
-def route(tokens_in, norm_moe, w_router, route_ids):
-    normed = rms_norm(tokens_in, norm_moe)
-    logits = jnp.dot(normed, w_router, preferred_element_type=jnp.float32)
-    picked = jnp.take_along_axis(logits, route_ids, axis=1)
-    return normed, jax.nn.softmax(picked, axis=-1)
 
 
 def expert_ffn(rows_in, expert_gate, expert_up, expert_down):
@@ -71,29 +65,57 @@
     rep_two = P(None, None)
     rep_three = P(None, None, None)
     expert_spec = P('ep', None, None)
+    chips = group_size // 2
+    same_core = [[2 * c for c in range(chips)], [2 * c + 1 for c in range(chips)]]
+    partner = [(i, i ^ 1) for i in range(group_size)]
 
     def local_program(resid_in, expert_idx, expert_slot, w_query, w_key, w_value, w_out, w_gate, w_up, w_down, w_router, norm_attn, norm_ffn, norm_moe, expert_gate, expert_up, expert_down):
         micro_count, seqs, seq_len, width = resid_in.shape
         tokens = seqs * seq_len
         choices = expert_idx.shape[-1]
         local_experts = expert_gate.shape[0]
-        capacity = CAP_FACTOR * tokens * choices // (local_experts * group_size)
-        buf_rows = local_experts * group_size * capacity
-        token_of_copy = jnp.broadcast_to(jnp.arange(tokens, dtype=jnp.int32)[:, None], (tokens, choices)).reshape(-1)
+        experts = local_experts * group_size
+        capacity = CAP_FACTOR * tokens * choices // experts
+        me = lax.axis_index('ep')
+        gate_all = jnp.stack([expert_gate, lax.ppermute(expert_gate, 'ep', partner)])
+        up_all = jnp.stack([expert_up, lax.ppermute(expert_up, 'ep', partner)])
+        down_all = jnp.stack([expert_down, lax.ppermute(expert_down, 'ep', partner)])
+        own_first = me * local_experts
+        other_first = (me ^ 1) * local_experts
+
+        def mine(table, axis):
+            return jnp.concatenate([lax.dynamic_slice_in_dim(table, own_first, local_experts, axis), lax.dynamic_slice_in_dim(table, other_first, local_experts, axis)], axis)
+
         outputs = []
         for micro in range(micro_count):
             resid = resid_in[micro]
-            route_ids = expert_idx[micro].reshape(tokens, choices)
-            route_slots = expert_slot[micro].reshape(tokens, choices)
-            normed, gates = route(resid.reshape(tokens, width), norm_moe, w_router, route_ids)
-            buf_pos = ((route_ids % local_experts) * group_size + route_ids // local_experts) * capacity + route_slots
-            source_row = jnp.full((buf_rows,), tokens, jnp.int32).at[buf_pos.reshape(-1)].set(token_of_copy)
-            send_buf = jnp.take(normed, source_row, axis=0, mode='fill', fill_value=0).reshape(local_experts, group_size, capacity, width)
-            received = lax.all_to_all(send_buf, 'ep', 1, 1, tiled=True)
-            expert_out = expert_ffn(received.reshape(local_experts, group_size * capacity, width), expert_gate, expert_up, expert_down)
-            returned = lax.all_to_all(expert_out.reshape(local_experts, group_size, capacity, width), 'ep', 1, 1, tiled=True)
-            per_copy = jnp.take(returned.reshape(buf_rows, width), buf_pos, axis=0)
-            moe_out = jnp.sum(gates[:, :, None] * per_copy.astype(jnp.float32), axis=1)
+            ids = expert_idx[micro].reshape(tokens, choices)
+            normed = rms_norm(resid.reshape(tokens, width), norm_moe)
+            logits = jnp.dot(normed, w_router, preferred_element_type=jnp.float32)
+            picked = jnp.any(ids[:, :, None] == jnp.arange(experts)[None, None, :], axis=1)
+            gates = jax.nn.softmax(jnp.where(picked, logits, NEG), axis=-1) * picked
+            lower = (jnp.arange(tokens)[:, None] >= jnp.arange(tokens)[None, :]).astype(jnp.bfloat16)
+            upto = jnp.dot(lower, picked.astype(jnp.bfloat16), preferred_element_type=jnp.float32)
+            tok_of = jnp.sum((upto.T[:, None, :] <= jnp.arange(capacity, dtype=jnp.float32)[None, :, None]).astype(jnp.int32), axis=-1)
+            all_tok = lax.all_gather(normed, 'ep', axis_index_groups=same_core)
+            all_tab = mine(lax.all_gather(tok_of, 'ep', axis_index_groups=same_core), 1)
+            all_gates = mine(lax.all_gather(gates, 'ep', axis_index_groups=same_core), 2)
+            all_upto = mine(lax.all_gather(jnp.where(picked, upto, 0.0), 'ep', axis_index_groups=same_core), 2)
+            row_tok = jnp.where(all_tab < tokens, all_tab + jnp.arange(chips)[:, None, None] * tokens, 0)
+            rows = jnp.take(all_tok.reshape(chips * tokens, width), row_tok.transpose(1, 0, 2).reshape(-1), axis=0)
+            rows = rows.reshape(2, local_experts, chips * capacity, width)
+            y = jnp.stack([expert_ffn(rows[0], gate_all[0], up_all[0], down_all[0]), expert_ffn(rows[1], gate_all[1], up_all[1], down_all[1])])
+            y = y.reshape(2 * local_experts * chips * capacity, width)
+            here = all_upto > 0
+            order = jnp.cumsum(here.astype(jnp.int32), axis=-1)
+            part = jnp.zeros((chips * tokens, width), jnp.float32)
+            row_id = (jnp.arange(2 * local_experts)[None, None, :] * chips + jnp.arange(chips)[:, None, None]) * capacity + all_upto.astype(jnp.int32) - 1
+            for j in range(choices):
+                hit = here & (order == j + 1)
+                rj = jnp.sum(jnp.where(hit, row_id, 0), axis=-1).reshape(-1)
+                gj = jnp.sum(jnp.where(hit, all_gates, 0.0), axis=-1).reshape(-1)
+                part = part + gj[:, None] * jnp.take(y, rj, axis=0).astype(jnp.float32)
+            moe_out = lax.psum_scatter(part.reshape(chips, tokens, width), 'ep', scatter_dimension=0, axis_index_groups=same_core)
             dense_out = dense_branch(resid, norm_attn, w_query, w_key, w_value, w_out, norm_ffn, w_gate, w_up, w_down)
             outputs.append((dense_out + moe_out.reshape(seqs, seq_len, width)).astype(jnp.bfloat16))
         return jnp.stack(outputs)

time: 4230 us -> 6070 us (1.43)
  local copies, waits for them, and re-layouts: 1480 us -> 3880 us
  waiting for transfers between devices: 861 us -> 8.44 us
  other arithmetic: 305 us -> 473 us
    gather x16 -> x14, local copies, waits for them, and re-layouts: 979 us -> 3730 us  [the longest x12 3440 us: local_program(): part = part + gj[:, None] * jnp.take(y, rj, axis=0).astype(jnp.float32)]
    all_to_all x4 -> x0, waiting for transfers between devices: 861 us -> none  [the longest x2 448 us: local_program(): lax.all_to_all(expert_out.reshape(local_experts, group_size, capacity, wi...]
    reshape x5 -> x14, local copies, waits for them, and re-layouts: 199 us -> 0.44 us  [the longest x2 0.26 us: local_program(): row_tok.transpose(1, 0, 2).reshape(-1)]
    all_to_all x4 -> x0, local copies, waits for them, and re-layouts: 198 us -> none  [the longest x2 99 us: local_program(): received = lax.all_to_all(send_buf, 'ep', 1, 1, tiled=True)]
    add x0 -> x2, other arithmetic: none -> 128 us  [local_program(): part = part + gj[:, None] * jnp.take(y, rj, axis=0).astype(jnp.float32)]
    another operation x1 -> x5, other arithmetic: 27.4 us -> 128 us  [the longest x2 100 us: local_program(): jnp.stack([expert_ffn(rows[0], gate_all[0], up_all[0], down_all[0]), expe...]
    slice x4 -> x2, local copies, waits for them, and re-layouts: 1.17 us -> 98.2 us  [local_program(): rows[0]]
    reduce_sum x5 -> x8, other arithmetic: 135 us -> 53.7 us  [the longest x2 31.4 us: local_program(): jnp.sum((upto.T[:, None, :] <= jnp.arange(capacity, dtype=jnp.float32)[No...]
  transfers between devices with their start and end apart: 4 -> 11, of which waited for: 4 -> 1; matrix products, arithmetic and copies ran while one was open for 57% -> 65% of each run, Pallas kernels for 0% -> 0%
where the time goes in v1:
time: 6070 us; the launch traced here: 5990 us
  local copies, waits for them, and re-layouts  3880 us (64%)
  matrix products  1590 us (26%)
  other arithmetic  473 us (8%)
    gather x12, local copies, waits for them, and re-layouts, local_program(): part = part + gj[:, None] * jnp.take(y, rj, axis=0).astype(jnp.float32)  3440 us
    dot_general x4, matrix products, expert_ffn(): jnp.einsum('lrd,ldf->lrf', rows_in, expert_up, preferred_element_type=jnp...  297 us
    gather x2, local copies, waits for them, and re-layouts, local_program(): jnp.take(all_tok.reshape(chips * tokens, width), row_tok.transpose(1, 0,...  296 us
    dot_general x4, matrix products, expert_ffn(): jnp.einsum('lrf,lfd->lrd', hidden, expert_down, preferred_element_type=jn...  277 us
    dot_general x4, matrix products, expert_ffn(): jnp.einsum('lrd,ldf->lrf', rows_in, expert_gate, preferred_element_type=j...  268 us
    dot_general x2, matrix products, dense_branch(): jnp.einsum('bsd,df->bsf', normed_ffn, w_gate, preferred_element_type=jnp....  178 us
    dot_general x2, matrix products, dense_branch(): jnp.einsum('bsf,fd->bsd', hidden, w_down, preferred_element_type=jnp.floa...  170 us
    dot_general x2, matrix products, dense_branch(): jnp.einsum('bsd,df->bsf', normed_ffn, w_up, preferred_element_type=jnp.fl...  159 us
  transfers between devices with their start and end apart: 11, of which 1 were waited for; matrix products, arithmetic and copies ran while one was open for 65% of the time, Pallas kernels for 0%

profile of v1, /device:TPU:0, one launch (start us, length us, event | category | flops | bytes accessed | tf_op | source)
XLA Modules:
  0.0 5993.7 jit_solution(7233943174521964709)
XLA Ops:
  7.3 6.3 fusion.64
  14.8 8.4 fusion.53
  35.9 10.4 fusion.60
  47.8 15.8 convert_reduce_fusion.1
  63.5 12.1 all-gather.2
  75.6 15.7 convert_reduce_fusion
  91.3 12.3 all-gather.5
  105.3 6.4 fusion.65
  111.6 12.4 copy.119
  124.0 12.4 copy.118
  136.5 19.4 fusion.76
  156.0 22.1 fusion.74
  178.1 17.0 fusion.78
  195.1 17.1 fusion.80
  215.3 27.3 subtract_convert_fusion.2
  242.6 19.0 fusion.28
  261.6 31.6 fusion.22
  293.2 17.6 fusion.23
  354.3 7.0 all-gather.15.cloned.1.call-done
  361.4 147.9 %gather_fusion.7 = bf16[18432,2048]{1,0:T(8,128)(2,1)} fusion(bf16[6144,2048]{1,0:T(8,128)(2,1)} %bitcast.323, s32[18432]{0:T(1024)} %fusion.165), kind=kCustom, calls=%fused_computation.2.clone | custom fusion | bytes 151068672 | tf_op jit(solution)/shard_map/jit(_take)/gather | solution.py:105
  509.3 49.7 broadcast_select_fusion
  559.0 49.1 fusion.193
  608.1 67.2 %fusion.202 = f32[8,1152,1408]{2,1,0:T(8,128)} fusion(bf16[8,1152,2048]{2,1,0:T(8,128)(2,1)} %bitcast.331, bf16[8,2048,1408]{2,1,0:T(8,128)(2,1)} %param.34), kind=kOutput, calls=%fused_computation.336 | convolution fusion | flops 53150220288 | bytes 135790592 | tf_op jit(solution)/shard_map/lrd,ldf->lrf/dot_general | solution.py:55
  675.3 147.8 %gather_fusion = bf16[18432,2048]{1,0:T(8,128)(2,1)} fusion(bf16[6144,2048]{1,0:T(8,128)(2,1)} %bitcast.324, s32[18432]{0:T(1024)S(1)} %copy-done.5), kind=kCustom, calls=%fused_computation.clone | custom fusion | bytes 151068672 | tf_op jit(solution)/shard_map/jit(_take)/gather | solution.py:105
  823.1 74.4 %fusion.13.clone.2 = bf16[8,1152,1408]{2,1,0:T(8,128)(2,1)} fusion(bf16[8,1152,2048]{2,1,0:T(8,128)(2,1)} %bitcast.332, bf16[8,2048,1408]{2,1,0:T(8,128)(2,1)} %param.35, f32[8,1152,1408]{2,1,0:T(8,128)} %fusion.202), kind=kOutput, calls=%fused_computation.43.clone.clone.clone | convolution fusion | flops 53228077056 | bytes 161742848 | tf_op jit(solution)/shard_map/lrd,ldf->lrf/dot_general | solution.py:56
  897.5 49.7 broadcast_select_fusion.1
  947.2 69.2 %fusion.26 = bf16[1,8,1152,2048]{3,2,1,0:T(8,128)(2,1)} fusion(bf16[8,1408,2048]{2,1,0:T(8,128)(2,1)} %param.36, bf16[8,1152,1408]{2,1,0:T(8,128)(2,1)} %fusion.13.clone.2), kind=kOutput, calls=%fused_computation.58 | convolution fusion | flops 53169094656 | bytes 109838336 | tf_op jit(solution)/shard_map/lrf,lfd->lrd/dot_general | solution.py:58
  1016.4 67.2 %fusion.203 = f32[8,1152,1408]{2,1,0:T(8,128)} fusion(bf16[8,1152,2048]{2,1,0:T(8,128)(2,1)} %bitcast.329, bf16[8,2048,1408]{2,1,0:T(8,128)(2,1)} %collective-permute-done), kind=kOutput, calls=%fused_computation.337 | convolution fusion | flops 53150220288 | bytes 135790592 | tf_op jit(solution)/shard_map/lrd,ldf->lrf/dot_general | solution.py:55
  1083.6 74.0 %multiply_convert_fusion.19 = bf16[8,1152,1408]{2,1,0:T(8,128)(2,1)} fusion(f32[8,1152,1408]{2,1,0:T(8,128)} %fusion.203, bf16[8,1152,2048]{2,1,0:T(8,128)(2,1)} %bitcast.330, bf16[8,2048,1408]{2,1,0:T(8,128)(2,1)} %collective-permute-done.1), kind=kOutput, calls=%fused_computation.26.clone.clone | convolution fusion | flops 53228077056 | bytes 161742848 | tf_op jit(solution)/shard_map/lrd,ldf->lrf/dot_general | solution.py:56
  1157.5 69.4 %fusion.27 = bf16[1,8,1152,2048]{3,2,1,0:T(8,128)(2,1)} fusion(bf16[8,1408,2048]{2,1,0:T(8,128)(2,1)} %collective-permute-done.2, bf16[8,1152,1408]{2,1,0:T(8,128)(2,1)} %multiply_convert_fusion.19), kind=kOutput, calls=%fused_computation.59 | convolution fusion | flops 53169094656 | bytes 109838336 | tf_op jit(solution)/shard_map/lrf,lfd->lrd/dot_general | solution.py:58
  1227.0 50.1 pad_maximum_fusion.1
  1277.1 332.6 %gather_fusion.13 = bf16[6144,2048]{1,0:T(8,128)(2,1)} fusion(bf16[18432,2048]{1,0:T(8,128)(2,1)} %bitcast.58, s32[6144]{0:T(1024)S(1)} %copy-done.12), kind=kCustom, calls=%fused_computation.13.clone | custom fusion | bytes 50356224 | tf_op jit(solution)/shard_map/jit(_take)/gather | solution.py:117
  1609.7 332.2 %gather_fusion.12 = bf16[6144,2048]{1,0:T(8,128)(2,1)} fusion(bf16[18432,2048]{1,0:T(8,128)(2,1)} %bitcast.58, s32[6144]{0:T(1024)S(1)} %copy-done.13), kind=kCustom, calls=%fused_computation.12.clone | custom fusion | bytes 50356224 | tf_op jit(solution)/shard_map/jit(_take)/gather | solution.py:117
  1942.0 326.1 %gather_fusion.11 = bf16[6144,2048]{1,0:T(8,128)(2,1)} fusion(bf16[18432,2048]{1,0:T(8,128)(2,1)} %bitcast.58, s32[6144]{0:T(1024)S(1)} %copy-done.14), kind=kCustom, calls=%fused_computation.11.clone | custom fusion | bytes 50356224 | tf_op jit(solution)/shard_map/jit(_take)/gather | solution.py:117
  2268.1 309.2 %gather_fusion.10 = bf16[6144,2048]{1,0:T(8,128)(2,1)} fusion(bf16[18432,2048]{1,0:T(8,128)(2,1)} %bitcast.58, s32[6144]{0:T(1024)S(1)} %copy-done.15), kind=kCustom, calls=%fused_computation.10.clone | custom fusion | bytes 50356224 | tf_op jit(solution)/shard_map/jit(_take)/gather | solution.py:117
  2577.3 252.5 %gather_fusion.9 = bf16[6144,2048]{1,0:T(8,128)(2,1)} fusion(bf16[18432,2048]{1,0:T(8,128)(2,1)} %bitcast.58, s32[6144]{0:T(1024)S(1)} %copy-done.16), kind=kCustom, calls=%fused_computation.9.clone | custom fusion | bytes 50356224 | tf_op jit(solution)/shard_map/jit(_take)/gather | solution.py:117
  2829.9 183.6 %gather_fusion.8 = bf16[6144,2048]{1,0:T(8,128)(2,1)} fusion(bf16[18432,2048]{1,0:T(8,128)(2,1)} %bitcast.58, s32[6144]{0:T(1024)S(1)} %copy-done.17), kind=kCustom, calls=%fused_computation.8.clone | custom fusion | bytes 50356224 | tf_op jit(solution)/shard_map/jit(_take)/gather | solution.py:117
  3013.7 63.8 %multiply_add_fusion = f32[6144,2048]{1,0:T(8,128)} fusion(bf16[6144,2048]{1,0:T(8,128)(2,1)} %gather_fusion.13, bf16[6144,2048]{1,0:T(8,128)(2,1)} %gather_fusion.12, bf16[6144,2048]{1,0:T(8,128)(2,1)} %gather_fusion.11, bf16[6144,2048]{1,0:T(8,128)(2,1)} %gather_fusion.10, bf16[6144,2048]{1,0:T(8,128)(2,1)} %gather_fusion.9, ...), kind=kLoop, calls=%fused_computation.28 | loop fusion | flops 289406976 | bytes 201510912 | tf_op jit(solution)/shard_map/add | solution.py:117
  3077.6 49.1 fusion.192
  3126.7 67.0 %fusion.200 = f32[8,1152,1408]{2,1,0:T(8,128)} fusion(bf16[8,1152,2048]{2,1,0:T(8,128)(2,1)} %bitcast.335, bf16[8,2048,1408]{2,1,0:T(8,128)(2,1)} %param.34), kind=kOutput, calls=%fused_computation.334 | convolution fusion | flops 53150220288 | bytes 135790592 | tf_op jit(solution)/shard_map/lrd,ldf->lrf/dot_general | solution.py:55
  3193.7 74.1 %fusion.12.clone.4 = bf16[8,1152,1408]{2,1,0:T(8,128)(2,1)} fusion(bf16[8,1152,2048]{2,1,0:T(8,128)(2,1)} %bitcast.336, bf16[8,2048,1408]{2,1,0:T(8,128)(2,1)} %param.35, f32[8,1152,1408]{2,1,0:T(8,128)} %fusion.200), kind=kOutput, calls=%fused_computation.42.clone.clone.clone.1 | convolution fusion | flops 53228077056 | bytes 161742848 | tf_op jit(solution)/shard_map/lrd,ldf->lrf/dot_general | solution.py:56
  3267.8 69.5 %fusion.24 = bf16[1,8,1152,2048]{3,2,1,0:T(8,128)(2,1)} fusion(bf16[8,1408,2048]{2,1,0:T(8,128)(2,1)} %param.36, bf16[8,1152,1408]{2,1,0:T(8,128)(2,1)} %fusion.12.clone.4), kind=kOutput, calls=%fused_computation.56 | convolution fusion | flops 53169094656 | bytes 109838336 | tf_op jit(solution)/shard_map/lrf,lfd->lrd/dot_general | solution.py:58
  3337.2 67.0 %fusion.201 = f32[8,1152,1408]{2,1,0:T(8,128)} fusion(bf16[8,1152,2048]{2,1,0:T(8,128)(2,1)} %bitcast.333, bf16[8,2048,1408]{2,1,0:T(8,128)(2,1)} %collective-permute-done), kind=kOutput, calls=%fused_computation.335 | convolution fusion | flops 53150220288 | bytes 135790592 | tf_op jit(solution)/shard_map/lrd,ldf->lrf/dot_general | solution.py:55
  3404.2 74.2 %multiply_convert_fusion.18 = bf16[8,1152,1408]{2,1,0:T(8,128)(2,1)} fusion(f32[8,1152,1408]{2,1,0:T(8,128)} %fusion.201, bf16[8,1152,2048]{2,1,0:T(8,128)(2,1)} %bitcast.334, bf16[8,2048,1408]{2,1,0:T(8,128)(2,1)} %collective-permute-done.1), kind=kOutput, calls=%fused_computation.27.clone.clone.1 | convolution fusion | flops 53228077056 | bytes 161742848 | tf_op jit(solution)/shard_map/lrd,ldf->lrf/dot_general | solution.py:56
  3478.5 69.2 %fusion.25 = bf16[1,8,1152,2048]{3,2,1,0:T(8,128)(2,1)} fusion(bf16[8,1408,2048]{2,1,0:T(8,128)(2,1)} %collective-permute-done.2, bf16[8,1152,1408]{2,1,0:T(8,128)(2,1)} %multiply_convert_fusion.18), kind=kOutput, calls=%fused_computation.57 | convolution fusion | flops 53169094656 | bytes 109838336 | tf_op jit(solution)/shard_map/lrf,lfd->lrd/dot_general | solution.py:58
  3547.7 50.1 pad_maximum_fusion
  3597.8 332.7 %gather_fusion.6 = bf16[6144,2048]{1,0:T(8,128)(2,1)} fusion(bf16[18432,2048]{1,0:T(8,128)(2,1)} %bitcast.29, s32[6144]{0:T(1024)S(1)} %copy-done.6), kind=kCustom, calls=%fused_computation.7.clone | custom fusion | bytes 50356224 | tf_op jit(solution)/shard_map/jit(_take)/gather | solution.py:117
  3930.6 330.1 %gather_fusion.5 = bf16[6144,2048]{1,0:T(8,128)(2,1)} fusion(bf16[18432,2048]{1,0:T(8,128)(2,1)} %bitcast.29, s32[6144]{0:T(1024)S(1)} %copy-done.7), kind=kCustom, calls=%fused_computation.6.clone | custom fusion | bytes 50356224 | tf_op jit(solution)/shard_map/jit(_take)/gather | solution.py:117
  4260.7 323.5 %gather_fusion.4 = bf16[6144,2048]{1,0:T(8,128)(2,1)} fusion(bf16[18432,2048]{1,0:T(8,128)(2,1)} %bitcast.29, s32[6144]{0:T(1024)S(1)} %copy-done.8), kind=kCustom, calls=%fused_computation.5.clone | custom fusion | bytes 50356224 | tf_op jit(solution)/shard_map/jit(_take)/gather | solution.py:117
  4584.2 305.0 %gather_fusion.3 = bf16[6144,2048]{1,0:T(8,128)(2,1)} fusion(bf16[18432,2048]{1,0:T(8,128)(2,1)} %bitcast.29, s32[6144]{0:T(1024)S(1)} %copy-done.9), kind=kCustom, calls=%fused_computation.4.clone | custom fusion | bytes 50356224 | tf_op jit(solution)/shard_map/jit(_take)/gather | solution.py:117
  4889.2 242.9 %gather_fusion.2 = bf16[6144,2048]{1,0:T(8,128)(2,1)} fusion(bf16[18432,2048]{1,0:T(8,128)(2,1)} %bitcast.29, s32[6144]{0:T(1024)S(1)} %copy-done.10), kind=kCustom, calls=%fused_computation.3.clone | custom fusion | bytes 50356224 | tf_op jit(solution)/shard_map/jit(_take)/gather | solution.py:117
  5132.2 165.0 %gather_fusion.1 = bf16[6144,2048]{1,0:T(8,128)(2,1)} fusion(bf16[18432,2048]{1,0:T(8,128)(2,1)} %bitcast.29, s32[6144]{0:T(1024)S(1)} %copy-done.11), kind=kCustom, calls=%fused_computation.1.clone | custom fusion | bytes 50356224 | tf_op jit(solution)/shard_map/jit(_take)/gather | solution.py:117
  5297.3 63.8 %multiply_add_fusion.1 = f32[6144,2048]{1,0:T(8,128)} fusion(bf16[6144,2048]{1,0:T(8,128)(2,1)} %gather_fusion.6, bf16[6144,2048]{1,0:T(8,128)(2,1)} %gather_fusion.5, bf16[6144,2048]{1,0:T(8,128)(2,1)} %gather_fusion.4, bf16[6144,2048]{1,0:T(8,128)(2,1)} %gather_fusion.3, bf16[6144,2048]{1,0:T(8,128)(2,1)} %gather_fusion.2, ...), kind=kLoop, calls=%fused_computation.29 | loop fusion | flops 289406976 | bytes 201510912 | tf_op jit(solution)/shard_map/add | solution.py:117
  5362.2 32.1 fusion.34
  5394.2 21.3 fusion.45
  5416.2 31.8 fusion.36
  5448.0 19.8 fusion.40
  5467.9 80.6 %fusion.4 = f32[4,384,10944]{1,2,0:T(8,128)} fusion(bf16[2048,10944]{0,1:T(8,128)(2,1)} %param.28, bf16[4,384,2048]{2,1,0:T(8,128)(2,1)S(1)} %copy-done.59, f32[4,384]{1,0:T(4,128)S(1)} %copy-done.50, f32[2048]{0:T(1024)S(1)} %copy-done.49), kind=kOutput, calls=%fused_computation.34 | convolution fusion | flops 68866277376 | bytes 118372352 | tf_op jit(solution)/shard_map/bsd,df->bsf/dot_general | solution.py:48
  5548.5 78.8 %fusion.6 = f32[4,384,10944]{1,2,0:T(8,128)} fusion(bf16[2048,10944]{0,1:T(8,128)(2,1)} %param.28, bf16[4,384,2048]{2,1,0:T(8,128)(2,1)S(1)} %get-tuple-element.115, f32[2048]{0:T(1024)S(1)} %copy-done.49, f32[4,384]{1,0:T(4,128)S(1)} %add_rsqrt_fusion.4), kind=kOutput, calls=%fused_computation.36 | convolution fusion | flops 68866277376 | bytes 118372352 | tf_op jit(solution)/shard_map/bsd,df->bsf/dot_general | solution.py:48
  5627.3 89.0 %multiply_convert_fusion.20 = bf16[4,384,10944]{1,2,0:T(8,128)(2,1)} fusion(f32[4,384,10944]{1,2,0:T(8,128)} %fusion.4, bf16[2048,10944]{0,1:T(8,128)(2,1)} %param.27, bf16[4,384,2048]{2,1,0:T(8,128)(2,1)} %get-tuple-element.113, f32[4,384]{1,0:T(4,128)S(1)} %copy-done.50, f32[2048]{0:T(1024)S(1)} %copy-done.49), kind=kOutput, calls=%fused_computation.24.clone.clone.clone.clone.1 | convolution fusion | flops 68967137280 | bytes 151992320 | tf_op jit(solution)/shard_map/bsd,df->bsf/dot_general | solution.py:47
  5716.3 89.2 %multiply_convert_fusion.21 = bf16[4,384,10944]{1,2,0:T(8,128)(2,1)} fusion(f32[4,384,10944]{1,2,0:T(8,128)} %fusion.6, bf16[2048,10944]{0,1:T(8,128)(2,1)} %param.27, bf16[4,384,2048]{2,1,0:T(8,128)(2,1)} %copy-done.60, f32[2048]{0:T(1024)S(1)} %copy-done.49, f32[4,384]{1,0:T(4,128)S(1)} %copy-done.52), kind=kOutput, calls=%fused_computation.25.clone.clone.clone.clone.1 | convolution fusion | flops 68967137280 | bytes 151992320 | tf_op jit(solution)/shard_map/bsd,df->bsf/dot_general | solution.py:47
  5805.5 85.2 %fusion.90 = bf16[1,4,384,2048]{3,2,1,0:T(8,128)(2,1)} fusion(f32[4,384,2048]{2,1,0:T(8,128)} %bitcast.345, bf16[4,384,2048]{2,1,0:T(8,128)(2,1)} %get-tuple-element.113, bf16[10944,2048]{1,0:T(8,128)(2,1)} %param.29, bf16[4,384,10944]{1,2,0:T(8,128)(2,1)} %multiply_convert_fusion.20), kind=kOutput, calls=%fused_computation.142 | convolution fusion | flops 68866277376 | bytes 103612416 | tf_op jit(solution)/shard_map/bsf,fd->bsd/dot_general | solution.py:50
  5890.7 85.2 %fusion.91 = bf16[1,4,384,2048]{3,2,1,0:T(8,128)(2,1)} fusion(f32[4,384,2048]{2,1,0:T(8,128)} %bitcast.346, bf16[4,384,2048]{2,1,0:T(8,128)(2,1)} %copy-done.60, bf16[10944,2048]{1,0:T(8,128)(2,1)} %param.29, bf16[4,384,10944]{1,2,0:T(8,128)(2,1)} %multiply_convert_fusion.21), kind=kOutput, calls=%fused_computation.143 | convolution fusion | flops 68866277376 | bytes 103612416 | tf_op jit(solution)/shard_map/bsf,fd->bsd/dot_general | solution.py:50
  5975.9 10.5 pad_maximum_fusion.2
  (275 shorter events, 65.9 us)
Async XLA Ops:
  6.5 304.2 %all-gather.19.cloned.1.call-start = ((), (), s32[]{:S(2)}) async-start(), calls=%async_computation.5 | async-start | bytes 1966080 | tf_op jit(solution)/shard_map/all_gather | solution.py:102
  27.2 286.2 %all-gather.17.cloned.1.call-start = ((), (), s32[]{:S(2)}) async-start(), calls=%async_computation.4 | async-start | bytes 1966080 | tf_op jit(solution)/shard_map/all_gather | solution.py:103
  28.0 288.6 %all-gather.23.cloned.1.call-start = ((), (), s32[]{:S(2)}) async-start(), calls=%async_computation.7 | async-start | bytes 1966080 | tf_op jit(solution)/shard_map/all_gather | solution.py:102
  35.2 284.5 %all-gather.21.cloned.1.call-start = ((), (), s32[]{:S(2)}) async-start(), calls=%async_computation.6 | async-start | bytes 1966080 | tf_op jit(solution)/shard_map/all_gather | solution.py:103
  35.8 325.6 %all-gather.15.cloned.1.call-start = ((), (), s32[]{:S(2)}) async-start(), calls=%async_computation.3 | async-start | bytes 31457280 | tf_op jit(solution)/shard_map/all_gather | solution.py:100
  46.2 77.8 %copy-start.57 = (bf16[2048]{0:T(1024)(128)(2,1)S(1)}, bf16[2048]{0:T(1024)(128)(2,1)}, u32[]{:S(2)}) copy-start(bf16[2048]{0:T(1024)(128)(2,1)} %param.31) | copy-start | bytes 12292
  46.2 629.1 %all-gather.13.cloned.1.call-start = ((), (), s32[]{:S(2)}) async-start(), calls=%async_computation.2 | async-start | bytes 31457280 | tf_op jit(solution)/shard_map/all_gather | solution.py:100
  46.3 1111.3 %collective-permute-start.2 = (bf16[8,1408,2048]{2,1,0:T(8,128)(2,1)}, bf16[8,1408,2048]{2,1,0:T(8,128)(2,1)}, u32[]{:S(2)}, u32[]{:S(2)}) collective-permute-start(bf16[8,1408,2048]{2,1,0:T(8,128)(2,1)} %param.36), channel_id=1, source_target_pairs={{0,1},{1,0},{2,3},{3,2},{4,5},{5,4},{6,7},{7,6}} | collective-permute-start | bytes 138412032 | tf_op jit(solution)/shard_map/ppermute | solution.py:82
  47.2 969.2 %collective-permute-start = (bf16[8,2048,1408]{2,1,0:T(8,128)(2,1)}, bf16[8,2048,1408]{2,1,0:T(8,128)(2,1)}, u32[]{:S(2)}, u32[]{:S(2)}) collective-permute-start(bf16[8,2048,1408]{2,1,0:T(8,128)(2,1)} %param.34), channel_id=1, source_target_pairs={{0,1},{1,0},{2,3},{3,2},{4,5},{5,4},{6,7},{7,6}} | collective-permute-start | bytes 138412032 | tf_op jit(solution)/shard_map/ppermute | solution.py:80
  47.2 1036.4 %collective-permute-start.1 = (bf16[8,2048,1408]{2,1,0:T(8,128)(2,1)}, bf16[8,2048,1408]{2,1,0:T(8,128)(2,1)}, u32[]{:S(2)}, u32[]{:S(2)}) collective-permute-start(bf16[8,2048,1408]{2,1,0:T(8,128)(2,1)} %param.35), channel_id=1, source_target_pairs={{0,1},{1,0},{2,3},{3,2},{4,5},{5,4},{6,7},{7,6}} | collective-permute-start | bytes 138412032 | tf_op jit(solution)/shard_map/ppermute | solution.py:81
  47.7 5757.8 %reduce-scatter.9.cloned.1.call-start = ((), (), s32[]{:S(2)}) async-start(), calls=%async_computation.9 | async-start | bytes 62914560
  105.2 188.0 %copy-start.3 = (pred[384,384]{0,1:T(8,128)(4,1)}, pred[384,384]{0,1:T(8,128)(4,1)S(1)}, u32[]{:S(2)}) copy-start(pred[384,384]{0,1:T(8,128)(4,1)S(1)} %iota_compare_fusion.7) | copy-start | bytes 442372
  124.0 71.1 %copy-start.47 = (f32[2048]{0:T(1024)}, f32[2048]{0:T(1024)S(1)}, u32[]{:S(2)}) copy-start(f32[2048]{0:T(1024)S(1)} %convert_element_type.254) | copy-start | bytes 24580
  136.5 41.6 copy-start.55
  136.5 58.6 copy-start.53
  136.5 41.6 slice-start
  136.5 41.6 slice-start.1
  136.5 41.6 slice-start.3
  155.9 22.2 slice-start.2
  293.2 22.8 copy-start.18
  361.4 147.9 %copy-start.33 = (pred[18432]{0:T(1024)(128)(4,1)S(1)}, pred[18432]{0:T(1024)(128)(4,1)}, u32[]{:S(2)}) copy-start(pred[18432]{0:T(1024)(128)(4,1)} %compare_and_fusion.12) | copy-start | bytes 55300
  608.1 67.2 %copy-start.5 = (s32[18432]{0:T(1024)S(1)}, s32[18432]{0:T(1024)}, u32[]{:S(2)}) copy-start(s32[18432]{0:T(1024)} %fusion.164) | copy-start | bytes 221188
  823.1 74.4 %copy-start.34 = (pred[18432]{0:T(1024)(128)(4,1)S(1)}, pred[18432]{0:T(1024)(128)(4,1)}, u32[]{:S(2)}) copy-start(pred[18432]{0:T(1024)(128)(4,1)} %compare_and_fusion.13) | copy-start | bytes 55300
  1227.0 50.1 copy-start.12
  1277.1 332.6 %copy-start.13 = (s32[6144]{0:T(1024)S(1)}, s32[6144]{0:T(1024)}, u32[]{:S(2)}) copy-start(s32[6144]{0:T(1024)} %fusion.176) | copy-start | bytes 73732
  1609.7 332.3 %copy-start.14 = (s32[6144]{0:T(1024)S(1)}, s32[6144]{0:T(1024)}, u32[]{:S(2)}) copy-start(s32[6144]{0:T(1024)} %fusion.175) | copy-start | bytes 73732
  1942.0 326.1 %copy-start.15 = (s32[6144]{0:T(1024)S(1)}, s32[6144]{0:T(1024)}, u32[]{:S(2)}) copy-start(s32[6144]{0:T(1024)} %fusion.174) | copy-start | bytes 73732
  2268.1 309.2 %copy-start.16 = (s32[6144]{0:T(1024)S(1)}, s32[6144]{0:T(1024)}, u32[]{:S(2)}) copy-start(s32[6144]{0:T(1024)} %fusion.173) | copy-start | bytes 73732
  2577.3 252.5 %copy-start.17 = (s32[6144]{0:T(1024)S(1)}, s32[6144]{0:T(1024)}, u32[]{:S(2)}) copy-start(s32[6144]{0:T(1024)} %fusion.172) | copy-start | bytes 73732
  2829.8 183.8 %copy-start.27 = (f32[6144]{0:T(1024)S(1)}, f32[6144]{0:T(1024)}, u32[]{:S(2)}) copy-start(f32[6144]{0:T(1024)} %mul.750) | copy-start | bytes 73732
  2829.8 183.8 %copy-start.28 = (f32[6144]{0:T(1024)S(1)}, f32[6144]{0:T(1024)}, u32[]{:S(2)}) copy-start(f32[6144]{0:T(1024)} %mul.747) | copy-start | bytes 73732
  2829.8 183.8 %copy-start.29 = (f32[6144]{0:T(1024)S(1)}, f32[6144]{0:T(1024)}, u32[]{:S(2)}) copy-start(f32[6144]{0:T(1024)} %mul.744) | copy-start | bytes 73732
  2829.8 183.8 %copy-start.30 = (f32[6144]{0:T(1024)S(1)}, f32[6144]{0:T(1024)}, u32[]{:S(2)}) copy-start(f32[6144]{0:T(1024)} %mul.741) | copy-start | bytes 73732
  2829.8 183.8 %copy-start.31 = (f32[6144]{0:T(1024)S(1)}, f32[6144]{0:T(1024)}, u32[]{:S(2)}) copy-start(f32[6144]{0:T(1024)} %mul.738) | copy-start | bytes 73732
  2829.9 183.8 %copy-start.32 = (f32[6144]{0:T(1024)S(1)}, f32[6144]{0:T(1024)}, u32[]{:S(2)}) copy-start(f32[6144]{0:T(1024)} %mul.728) | copy-start | bytes 73732
  2829.9 183.8 %copy-start.41 = (pred[6144]{0:T(1024)(128)(4,1)S(1)}, pred[6144]{0:T(1024)(128)(4,1)}, u32[]{:S(2)}) copy-start(pred[6144]{0:T(1024)(128)(4,1)} %compare_and_fusion.14) | copy-start | bytes 18436
  2829.9 183.8 %copy-start.42 = (pred[6144]{0:T(1024)(128)(4,1)S(1)}, pred[6144]{0:T(1024)(128)(4,1)}, u32[]{:S(2)}) copy-start(pred[6144]{0:T(1024)(128)(4,1)} %compare_and_fusion.15) | copy-start | bytes 18436
  2829.9 183.8 %copy-start.43 = (pred[6144]{0:T(1024)(128)(4,1)S(1)}, pred[6144]{0:T(1024)(128)(4,1)}, u32[]{:S(2)}) copy-start(pred[6144]{0:T(1024)(128)(4,1)} %compare_and_fusion.16) | copy-start | bytes 18436
  2829.9 183.8 %copy-start.44 = (pred[6144]{0:T(1024)(128)(4,1)S(1)}, pred[6144]{0:T(1024)(128)(4,1)}, u32[]{:S(2)}) copy-start(pred[6144]{0:T(1024)(128)(4,1)} %compare_and_fusion.17) | copy-start | bytes 18436
  2829.9 183.8 %copy-start.45 = (pred[6144]{0:T(1024)(128)(4,1)S(1)}, pred[6144]{0:T(1024)(128)(4,1)}, u32[]{:S(2)}) copy-start(pred[6144]{0:T(1024)(128)(4,1)} %compare_and_fusion.18) | copy-start | bytes 18436
  2829.9 183.8 %copy-start.46 = (pred[6144]{0:T(1024)(128)(4,1)S(1)}, pred[6144]{0:T(1024)(128)(4,1)}, u32[]{:S(2)}) copy-start(pred[6144]{0:T(1024)(128)(4,1)} %compare_and_fusion.19) | copy-start | bytes 18436
  3077.5 2813.1 %reduce-scatter.7.cloned.1.call-start = ((), (), s32[]{:S(2)}) async-start(), calls=%async_computation.8 | async-start | bytes 62914560
  3547.7 50.1 copy-start.6
  3597.8 332.7 %copy-start.7 = (s32[6144]{0:T(1024)S(1)}, s32[6144]{0:T(1024)}, u32[]{:S(2)}) copy-start(s32[6144]{0:T(1024)} %fusion.170) | copy-start | bytes 73732
  3930.6 330.1 %copy-start.8 = (s32[6144]{0:T(1024)S(1)}, s32[6144]{0:T(1024)}, u32[]{:S(2)}) copy-start(s32[6144]{0:T(1024)} %fusion.169) | copy-start | bytes 73732
  4260.7 323.5 %copy-start.9 = (s32[6144]{0:T(1024)S(1)}, s32[6144]{0:T(1024)}, u32[]{:S(2)}) copy-start(s32[6144]{0:T(1024)} %fusion.168) | copy-start | bytes 73732
  4584.2 305.0 %copy-start.10 = (s32[6144]{0:T(1024)S(1)}, s32[6144]{0:T(1024)}, u32[]{:S(2)}) copy-start(s32[6144]{0:T(1024)} %fusion.167) | copy-start | bytes 73732
  4889.2 242.9 %copy-start.11 = (s32[6144]{0:T(1024)S(1)}, s32[6144]{0:T(1024)}, u32[]{:S(2)}) copy-start(s32[6144]{0:T(1024)} %fusion.166) | copy-start | bytes 73732
  5132.1 165.1 %copy-start.21 = (f32[6144]{0:T(1024)S(1)}, f32[6144]{0:T(1024)}, u32[]{:S(2)}) copy-start(f32[6144]{0:T(1024)} %mul.699) | copy-start | bytes 73732
  5132.1 165.1 %copy-start.22 = (f32[6144]{0:T(1024)S(1)}, f32[6144]{0:T(1024)}, u32[]{:S(2)}) copy-start(f32[6144]{0:T(1024)} %mul.696) | copy-start | bytes 73732
  5132.1 165.1 %copy-start.23 = (f32[6144]{0:T(1024)S(1)}, f32[6144]{0:T(1024)}, u32[]{:S(2)}) copy-start(f32[6144]{0:T(1024)} %mul.693) | copy-start | bytes 73732
  5132.1 165.1 %copy-start.24 = (f32[6144]{0:T(1024)S(1)}, f32[6144]{0:T(1024)}, u32[]{:S(2)}) copy-start(f32[6144]{0:T(1024)} %mul.690) | copy-start | bytes 73732
  5132.1 165.1 %copy-start.25 = (f32[6144]{0:T(1024)S(1)}, f32[6144]{0:T(1024)}, u32[]{:S(2)}) copy-start(f32[6144]{0:T(1024)} %mul.687) | copy-start | bytes 73732
  5132.1 165.1 %copy-start.26 = (f32[6144]{0:T(1024)S(1)}, f32[6144]{0:T(1024)}, u32[]{:S(2)}) copy-start(f32[6144]{0:T(1024)} %mul.673) | copy-start | bytes 73732
  5132.1 165.1 %copy-start.35 = (pred[6144]{0:T(1024)(128)(4,1)S(1)}, pred[6144]{0:T(1024)(128)(4,1)}, u32[]{:S(2)}) copy-start(pred[6144]{0:T(1024)(128)(4,1)} %compare_and_fusion.20) | copy-start | bytes 18436
  5132.1 165.1 %copy-start.36 = (pred[6144]{0:T(1024)(128)(4,1)S(1)}, pred[6144]{0:T(1024)(128)(4,1)}, u32[]{:S(2)}) copy-start(pred[6144]{0:T(1024)(128)(4,1)} %compare_and_fusion.21) | copy-start | bytes 18436
  5132.1 165.1 %copy-start.37 = (pred[6144]{0:T(1024)(128)(4,1)S(1)}, pred[6144]{0:T(1024)(128)(4,1)}, u32[]{:S(2)}) copy-start(pred[6144]{0:T(1024)(128)(4,1)} %compare_and_fusion.22) | copy-start | bytes 18436
  5132.2 165.1 %copy-start.38 = (pred[6144]{0:T(1024)(128)(4,1)S(1)}, pred[6144]{0:T(1024)(128)(4,1)}, u32[]{:S(2)}) copy-start(pred[6144]{0:T(1024)(128)(4,1)} %compare_and_fusion.23) | copy-start | bytes 18436
  5132.2 165.1 %copy-start.39 = (pred[6144]{0:T(1024)(128)(4,1)S(1)}, pred[6144]{0:T(1024)(128)(4,1)}, u32[]{:S(2)}) copy-start(pred[6144]{0:T(1024)(128)(4,1)} %compare_and_fusion.24) | copy-start | bytes 18436
  5132.2 165.1 %copy-start.40 = (pred[6144]{0:T(1024)(128)(4,1)S(1)}, pred[6144]{0:T(1024)(128)(4,1)}, u32[]{:S(2)}) copy-start(pred[6144]{0:T(1024)(128)(4,1)} %compare_and_fusion.25) | copy-start | bytes 18436
  5467.8 80.7 %copy-start.60 = (bf16[4,384,2048]{2,1,0:T(8,128)(2,1)}, bf16[4,384,2048]{2,1,0:T(8,128)(2,1)S(1)}, u32[]{:S(2)}) copy-start(bf16[4,384,2048]{2,1,0:T(8,128)(2,1)S(1)} %get-tuple-element.115) | copy-start | bytes 18874372
  5467.9 80.6 %copy-start.51 = (f32[4,384]{1,0:T(4,128)}, f32[4,384]{1,0:T(4,128)S(1)}, u32[]{:S(2)}) copy-start(f32[4,384]{1,0:T(4,128)S(1)} %add_rsqrt_fusion.4) | copy-start | bytes 18436
  5627.3 89.0 %copy-start.52 = (f32[4,384]{1,0:T(4,128)S(1)}, f32[4,384]{1,0:T(4,128)}, u32[]{:S(2)}) copy-start(f32[4,384]{1,0:T(4,128)} %copy-done.51) | copy-start | bytes 18436
  5890.7 95.7 %copy-start.1 = (bf16[2048,64]{0,1:T(8,128)(2,1)S(1)}, bf16[2048,64]{0,1:T(8,128)(2,1)}, u32[]{:S(2)}) copy-start(bf16[2048,64]{0,1:T(8,128)(2,1)} %param.30) | copy-start | bytes 786436
  (15 other events, 208.3 us)
Sparse Core Ops, SparseCore 0:
  27.3 27.8 all-gather.18
  57.0 25.6 all-gather.16
  84.5 26.3 all-gather.22
  112.5 24.9 all-gather.20
  139.2 222.1 all-gather.14
  363.0 222.1 all-gather.12
  3077.7 416.8 reduce-scatter.8
  5361.3 416.8 reduce-scatter.6
